TPU v7x, 32 devices: a whole 2x2x4 slice. The times are simulated.
32 devices in a mesh: rows: 8 (over y, x, core), cores: 4 (over z).
Axes of the slice: x: 2, y: 2, z: 4, core: 2. Of those that a mesh axis runs over, the one named last changes fastest.
Arguments:
- rhs: float32 [131072, 128], P(('rows', 'cores')), may hold values from -6 to 6
- guess: float32 [131072, 128], P(('rows', 'cores')), may hold values from -4 to 4
- degree: float32 [131072], P(('rows', 'cores')), may hold values from 2 to 6
- weights: bfloat16 [1024, 16, 128, 128], P(('rows', 'cores')), may hold values from -0.1875 to 0.1875
- columns: int32 [1024, 16], P(('rows', 'cores')), may hold values from 0 to 95, as said below
- block_counts: int32 [1024], P(('rows', 'cores')), may hold values from 8 to 16, as said below
- send_lists: int32 [32, 32, 2], P(('rows', 'cores')), may hold values from 0 to 31
- aggregates: int32 [131072], P(('rows', 'cores')), may hold values from 0 to 16383
- coarse_diag: float32 [16384], replicated, may hold values from 4 to 32
Outputs:
- smoothed: float32 [131072, 128], P(('rows', 'cores'))
Inputs may be any that keep to these rules, and one draw needn't show every extreme that they name: `block_counts`: every block row has 8 or 16 live slots, and the rows of one device have exactly 320 live slots in all. `columns`: on every device, each table index from 32 up is named by at least one live slot.
All inputs are finite; a program needn't handle non-finite values.
Results may differ from a plain program's by a relative error of at most 0.0022.
Values may be sent and summed in bfloat16 or wider, within the bound.
A program may use at most 128 MiB of HBM per device.

v0:
```python
import jax
import jax.numpy as jnp
from jax import lax
from jax.sharding import PartitionSpec as P

NC = 16384


damping = 0.7


def body(rhs, guess, degree, weights, columns, block_counts, send_lists, aggregates, coarse_diag):
    nblocks = weights.shape[0]
    slots = weights.shape[1]
    blocksize = weights.shape[2]
    width = rhs.shape[1]
    my_lists = send_lists[0]
    flat_live = jnp.arange(slots, dtype=jnp.int32)[None, :] < block_counts[:, None]
    live_weights = weights * flat_live.astype(jnp.bfloat16)[:, :, None, None]

    def apply(field):
        blocks = field.astype(jnp.bfloat16).reshape(nblocks, blocksize, width)
        outgoing = blocks[my_lists]
        incoming = lax.all_to_all(
            outgoing, ("rows", "cores"), split_axis=0, concat_axis=0, tiled=True
        )
        table = jnp.concatenate([blocks, incoming.reshape(-1, blocksize, width)], 0)
        offsum = jnp.einsum(
            "bsij,bsjr->bir", live_weights, table[columns], preferred_element_type=jnp.float32
        )
        return degree[:, None] * field - offsum.reshape(-1, width)

    first = guess + damping * (rhs - apply(guess)) / degree[:, None]
    residue = rhs - apply(first)
    local_coarse = jax.ops.segment_sum(residue, aggregates, num_segments=NC)
    total = lax.psum(local_coarse, ("rows", "cores"))
    correction = (total / coarse_diag[:, None]).astype(jnp.bfloat16)
    second = first + correction[aggregates].astype(jnp.float32)
    return second + damping * (rhs - apply(second)) / degree[:, None]


def solution(mesh):
    return jax.shard_map(
        body,
        mesh=mesh,
        in_specs=(
            P(("rows", "cores"), None),
            P(("rows", "cores"), None),
            P(("rows", "cores")),
            P(("rows", "cores"), None, None, None),
            P(("rows", "cores"), None),
            P(("rows", "cores")),
            P(("rows", "cores"), None, None),
            P(("rows", "cores")),
            P(),
        ),
        out_specs=P(("rows", "cores"), None),
        check_vma=False,
    )
```

profile of v0, /device:TPU:0, one launch (start us, length us, event | category | flops | bytes accessed | tf_op | source)
XLA Modules:
  0.0 500.1 jit_solution(2069053001239833863)
XLA Ops:
  6.5 0.7 compare_select_fusion.2
  7.2 0.1 copy.11
  7.3 0.1 reshape.90
  7.4 1.7 convert_element_type.23
  9.1 2.1 gather_fusion
  11.3 7.3 %all-to-all-start = ((bf16[32,2,128,128]{3,2,1,0:T(8,128)(2,1)}), bf16[32,2,128,128]{3,2,1,0:T(8,128)(2,1)S(1)}, u32[]{:S(2)}, u32[]{:S(2)}) async-start(bf16[32,2,128,128]{3,2,1,0:T(8,128)(2,1)} %bitcast.65), calls=%async_computation | async-start | bytes 4194304 | tf_op jit(solution)/shard_map/all_to_all | solution.py:24
  18.7 0.1 copy.12
  18.8 0.1 reshape.98
  18.9 0.1 fusion.22
  18.9 46.6 %all-to-all-done = bf16[32,2,128,128]{3,2,1,0:T(8,128)(2,1)S(1)} async-done(((bf16[32,2,128,128]{3,2,1,0:T(8,128)(2,1)}), bf16[32,2,128,128]{3,2,1,0:T(8,128)(2,1)S(1)}, u32[]{:S(2)}, u32[]{:S(2)}) %all-to-all-start) | async-done | bytes 2097184 | tf_op jit(solution)/shard_map/all_to_all | solution.py:24
  65.5 1.3 copy-done.11
  66.8 2.1 pad_maximum_fusion
  69.0 13.9 %gather_fusion.1 = bf16[512,128,128]{2,1,0:T(8,128)(2,1)} fusion(bf16[96,128,128]{2,1,0:T(8,128)(2,1)S(1)} %pad_maximum_fusion, s32[1024]{0:T(1024)S(1)} %pad_clamp_fusion), kind=kCustom, calls=%fused_computation.1 | custom fusion | bytes 33556480 | tf_op jit(solution)/shard_map/gather | solution.py:29
  82.9 13.1 %fusion.4 = f32[32,128,128,1]{2,1,3,0:T(8,128)S(1)} fusion(bf16[32,16,128,128]{3,2,1,0:T(8,128)(2,1)} %bitcast.58, bf16[32,16,128,128]{3,2,1,0:T(8,128)(2,1)} %param.12, bf16[32,16]{1,0:T(8,128)(2,1)S(1)} %fusion.22), kind=kOutput, calls=%fused_computation.12 | convolution fusion | flops 2155872256 | bytes 35652608 | tf_op jit(solution)/shard_map/bsij,bsjr->bir/dot_general | solution.py:28
  96.0 2.0 fusion.23
  98.0 0.9 gather_fusion.2
  99.0 51.8 %all_to_all.15 = bf16[32,2,128,128]{3,2,1,0:T(8,128)(2,1)S(1)} all-to-all(bf16[32,2,128,128]{3,2,1,0:T(8,128)(2,1)S(1)} %bitcast.67), channel_id=1, replica_groups=mesh['rows'=8,'cores'=4] {'rows','cores'}, dimensions={0} | all-to-all | bytes 4194304 | tf_op jit(solution)/shard_map/all_to_all | solution.py:24
  150.8 0.3 pad_maximum_fusion.1
  151.0 13.9 %gather_fusion.3 = bf16[512,128,128]{2,1,0:T(8,128)(2,1)} fusion(bf16[96,128,128]{2,1,0:T(8,128)(2,1)S(1)} %pad_maximum_fusion.1, s32[1024]{0:T(1024)S(1)} %pad_clamp_fusion), kind=kCustom, calls=%fused_computation.3 | custom fusion | bytes 33556480 | tf_op jit(solution)/shard_map/gather | solution.py:29
  165.0 13.1 %fusion.2 = f32[32,128,128,1]{2,1,3,0:T(8,128)S(1)} fusion(bf16[32,16,128,128]{3,2,1,0:T(8,128)(2,1)} %bitcast.59, bf16[32,16,128,128]{3,2,1,0:T(8,128)(2,1)} %param.12, bf16[32,16]{1,0:T(8,128)(2,1)S(1)} %fusion.22), kind=kOutput, calls=%fused_computation.10 | convolution fusion | flops 2155872256 | bytes 35652608 | tf_op jit(solution)/shard_map/bsij,bsjr->bir/dot_general | solution.py:28
  178.1 2.0 fusion.15
  180.1 26.4 %scatter_custom_fusion = f32[16384,128]{1,0:T(8,128)} fusion(s32[4096]{0:T(1024)S(1)} %copy-done.15, f32[4096,128]{1,0:T(8,128)} %fusion.15, f32[]{:T(128)} %constant.2.clone.1), kind=kCustom, calls=%fused_computation.18 | custom fusion | flops 524288 | bytes 8389120 | tf_op jit(solution)/shard_map/scatter-add | solution.py:35
  206.6 179.1 %all-reduce.2.cloned.1.call-done = f32[16384,128]{1,0:T(8,128)} async-done(((f32[16384,128]{1,0:T(8,128)}), f32[16384,128]{1,0:T(8,128)}) %all-reduce.2.cloned.1.call-update) | async-done | bytes 8388624 | tf_op jit(solution)/shard_map/psum | solution.py:36
  385.7 6.9 %divide_convert_fusion = bf16[16384,128]{1,0:T(8,128)(2,1)} fusion(f32[16384,128]{1,0:T(8,128)} %all-reduce.2.cloned.1.call-done, f32[16384]{0:T(1024)S(1)} %copy-done.14), kind=kLoop, calls=%fused_computation.14 | loop fusion | flops 4194304 | bytes 12648448 | tf_op jit(solution)/shard_map/convert_element_type | solution.py:37
  392.6 17.1 %gather_fusion.4 = bf16[4096,128]{1,0:T(8,128)(2,1)} fusion(bf16[16384,128]{1,0:T(8,128)(2,1)} %divide_convert_fusion, s32[4096]{0:T(1024)S(1)} %fusion.21), kind=kCustom, calls=%fused_computation.4 | custom fusion | bytes 2113536 | tf_op jit(solution)/shard_map/gather | solution.py:38
  409.6 1.4 fusion.20
  411.1 1.0 gather_fusion.5
  412.1 51.9 %all_to_all.16 = bf16[32,2,128,128]{3,2,1,0:T(8,128)(2,1)S(1)} all-to-all(bf16[32,2,128,128]{3,2,1,0:T(8,128)(2,1)S(1)} %bitcast.66), channel_id=1, replica_groups=mesh['rows'=8,'cores'=4] {'rows','cores'}, dimensions={0} | all-to-all | bytes 4194304 | tf_op jit(solution)/shard_map/all_to_all | solution.py:24
  463.9 0.3 pad_maximum_fusion.2
  464.2 13.9 %gather_fusion.6 = bf16[512,128,128]{2,1,0:T(8,128)(2,1)} fusion(bf16[96,128,128]{2,1,0:T(8,128)(2,1)S(1)} %pad_maximum_fusion.2, s32[1024]{0:T(1024)S(1)} %pad_clamp_fusion), kind=kCustom, calls=%fused_computation.6 | custom fusion | bytes 33556480 | tf_op jit(solution)/shard_map/gather | solution.py:29
  478.1 13.1 %fusion = f32[32,128,128,1]{2,1,3,0:T(8,128)S(1)} fusion(bf16[32,16,128,128]{3,2,1,0:T(8,128)(2,1)} %bitcast.57, bf16[32,16,128,128]{3,2,1,0:T(8,128)(2,1)} %param.12, bf16[32,16]{1,0:T(8,128)(2,1)S(1)} %fusion.22), kind=kOutput, calls=%fused_computation.8 | convolution fusion | flops 2155872256 | bytes 35652608 | tf_op jit(solution)/shard_map/bsij,bsjr->bir/dot_general | solution.py:28
  491.3 2.0 fusion.14
  (41 shorter events, 0.2 us)
Async XLA Ops:
  9.1 2.1 copy-start.5
  11.3 7.4 %copy-start.16 = (s32[32,16]{0,1:T(8,128)S(1)}, s32[32,16]{0,1:T(8,128)}, u32[]{:S(2)}) copy-start(s32[32,16]{0,1:T(8,128)} %param.13) | copy-start | bytes 6148
  11.3 7.6 %copy-start.17 = (s32[32]{0:T(128)S(1)}, s32[32]{0:T(128)}, u32[]{:S(2)}) copy-start(s32[32]{0:T(128)} %param.14) | copy-start | bytes 388
  11.3 54.2 %all-to-all-start = ((bf16[32,2,128,128]{3,2,1,0:T(8,128)(2,1)}), bf16[32,2,128,128]{3,2,1,0:T(8,128)(2,1)S(1)}, u32[]{:S(2)}, u32[]{:S(2)}) async-start(bf16[32,2,128,128]{3,2,1,0:T(8,128)(2,1)} %bitcast.65), calls=%async_computation | async-start | bytes 4194304 | tf_op jit(solution)/shard_map/all_to_all | solution.py:24
  18.6 367.1 %all-reduce.2.cloned.1.call-start = ((), (), s32[]{:S(2)}) async-start(), calls=%async_computation.3 | async-start | bytes 16777216 | tf_op jit(solution)/shard_map/psum | solution.py:36
  65.5 1.3 copy-start.11
  82.9 13.1 %copy-start.2 = (f32[4096,128]{1,0:T(8,128)S(1)}, f32[4096,128]{1,0:T(8,128)}, u32[]{:S(2)}) copy-start(f32[4096,128]{1,0:T(8,128)} %param.9) | copy-start | bytes 6291460
  82.9 13.1 %copy-start.12 = (f32[4096,128]{1,0:T(8,128)S(1)}, f32[4096,128]{1,0:T(8,128)}, u32[]{:S(2)}) copy-start(f32[4096,128]{1,0:T(8,128)} %param.10) | copy-start | bytes 6291460
  82.9 13.2 %copy-start.13 = (f32[4096]{0:T(1024)S(1)}, f32[4096]{0:T(1024)}, u32[]{:S(2)}) copy-start(f32[4096]{0:T(1024)} %param.11) | copy-start | bytes 49156
  98.0 1.0 copy-start.6
  99.0 51.8 %copy-start.7 = (bf16[4096,128]{1,0:T(8,128)(2,1)S(1)}, bf16[4096,128]{1,0:T(8,128)(2,1)}, u32[]{:S(2)}) copy-start(bf16[4096,128]{1,0:T(8,128)(2,1)} %copy-done.6) | copy-start | bytes 3145732
  165.0 13.1 %copy-start = (f32[4096,128]{1,0:T(8,128)S(1)}, f32[4096,128]{1,0:T(8,128)}, u32[]{:S(2)}) copy-start(f32[4096,128]{1,0:T(8,128)} %get-tuple-element.6) | copy-start | bytes 6291460
  165.0 13.1 %copy-start.3 = (f32[4096,128]{1,0:T(8,128)S(1)}, f32[4096,128]{1,0:T(8,128)}, u32[]{:S(2)}) copy-start(f32[4096,128]{1,0:T(8,128)} %param.9) | copy-start | bytes 6291460
  178.1 2.0 copy-start.15
  206.5 179.2 %copy-start.14 = (f32[16384]{0:T(1024)S(1)}, f32[16384]{0:T(1024)}, u32[]{:S(2)}) copy-start(f32[16384]{0:T(1024)} %param.17) | copy-start | bytes 196612
  411.1 1.0 copy-start.8
  412.1 51.9 %copy-start.9 = (bf16[4096,128]{1,0:T(8,128)(2,1)S(1)}, bf16[4096,128]{1,0:T(8,128)(2,1)}, u32[]{:S(2)}) copy-start(bf16[4096,128]{1,0:T(8,128)(2,1)} %copy-done.8) | copy-start | bytes 3145732
  478.1 13.1 %copy-start.1 = (f32[4096,128]{1,0:T(8,128)S(1)}, f32[4096,128]{1,0:T(8,128)}, u32[]{:S(2)}) copy-start(f32[4096,128]{1,0:T(8,128)} %get-tuple-element.6) | copy-start | bytes 6291460
  478.1 13.1 %copy-start.4 = (f32[4096,128]{1,0:T(8,128)S(1)}, f32[4096,128]{1,0:T(8,128)}, u32[]{:S(2)}) copy-start(f32[4096,128]{1,0:T(8,128)} %param.9) | copy-start | bytes 6291460
  478.1 13.1 %copy-start.10 = (bf16[4096,128]{1,0:T(8,128)(2,1)S(1)}, bf16[4096,128]{1,0:T(8,128)(2,1)}, u32[]{:S(2)}) copy-start(bf16[4096,128]{1,0:T(8,128)(2,1)} %gather_fusion.4) | copy-start | bytes 3145732
Sparse Core Ops, SparseCore 0:
  206.7 178.9 all-reduce.1
where the time goes:
time: 502 us; the launch traced here: 500 us
  waiting for transfers between devices  226 us (45%)
  blocking collectives  104 us (21%)
  local copies, waits for them, and re-layouts  64.6 us (13%)
  other arithmetic  45.8 us (9%)
  matrix products  39.3 us (8%)
  between operations  13.6 us (3%)
  starting transfers between devices  7.37 us (1%)
    psum x1, waiting for transfers between devices, body(): total = lax.psum(local_coarse, ('rows', 'cores'))  179 us
    all_to_all x2, blocking collectives, apply(): lax.all_to_all(outgoing, ('rows', 'cores'), split_axis=0, concat_axis=0,...  104 us
    all_to_all x1, waiting for transfers between devices, apply(): lax.all_to_all(outgoing, ('rows', 'cores'), split_axis=0, concat_axis=0,...  46.6 us
    gather x3, local copies, waits for them, and re-layouts, apply(): table[columns]  41.8 us
    dot_general x3, matrix products, apply(): jnp.einsum('bsij,bsjr->bir', live_weights, table[columns], preferred_elem...  39.3 us
    scatter-add x1, other arithmetic, body(): local_coarse = jax.ops.segment_sum(residue, aggregates, num_segments=NC)  26.4 us
    gather x1, local copies, waits for them, and re-layouts, body(): second = first + correction[aggregates].astype(jnp.float32)  17.1 us
  transfers between devices with their start and end apart: 2, of which 2 were waited for; matrix products, arithmetic and copies ran while one was open for 0% of the time, Pallas kernels for 0%

commit v1 on v0

v1 whole, which is shorter than its diff:
```python
import functools
import jax
import jax.numpy as jnp
from jax import lax
from jax.experimental import pallas as pl
from jax.experimental.pallas import tpu as pltpu
from jax.sharding import PartitionSpec as P

damping = 0.7
LIMIT = 64 * 1024 * 1024 - 65536
MESH = pl.DeviceIdType.MESH
VM = pl.BlockSpec(memory_space=pltpu.VMEM)
SM = pl.BlockSpec(memory_space=pltpu.SMEM)
ANY = pl.BlockSpec(memory_space=pl.ANY)
f32, bf16, i32 = jnp.float32, jnp.bfloat16, jnp.int32


def column_of(deg, b):
    row = deg[pl.ds(b, 1), :]
    return jnp.transpose(jnp.broadcast_to(row, (row.shape[1], row.shape[1])))


def half_product(w, tab, cols, b, first, count):
    left = jnp.concatenate([w[b, first + s] for s in range(count)], axis=1)
    right = jnp.concatenate([tab[cols[b, first + s]] for s in range(count)], axis=0)
    return jnp.dot(left, right, preferred_element_type=f32)


def relax_kernel(nr, nz, guess, rhs, deg, agg, cols, counts, sends, w_hbm,
                 x1, res, tab_out, hagg_out,
                 w, tab1, tab2, pack, aggpack, hagg, dcol,
                 wsem, osem, s1, r1, s2, r2, sa, ra):
    n = nr * nz
    nb, slots = w.shape[0], w.shape[1]
    mb = pack.shape[0] // n
    me = lax.axis_index("rows") * nz + lax.axis_index("cores")
    barrier = pltpu.get_barrier_semaphore()

    def where(t):
        return (t // nz, lax.rem(t, nz))

    @pl.loop(1, n)
    def _(k):
        pl.semaphore_signal(barrier, 1, device_id=where(lax.rem(me + k, n)), device_id_type=MESH)

    weights_copy = pltpu.make_async_copy(w_hbm, w, wsem)
    weights_copy.start()

    @pl.loop(0, n)
    def _(t):
        for j in range(mb):
            b = sends[t * mb + j]
            pack[t * mb + j] = guess[b].astype(bf16)
            aggpack[t, pl.ds(j, 1), :] = agg[pl.ds(b, 1), :]

    pl.semaphore_wait(barrier, n - 1)

    def data_copy(k, tab, ss, rr):
        t = lax.rem(me + k, n)
        return pltpu.make_async_remote_copy(
            src_ref=pack.at[pl.ds(t * mb, mb)], dst_ref=tab.at[pl.ds(nb + me * mb, mb)],
            send_sem=ss.at[k], recv_sem=rr.at[k], device_id=where(t), device_id_type=MESH)

    def agg_copy(k):
        t = lax.rem(me + k, n)
        return pltpu.make_async_remote_copy(
            src_ref=aggpack.at[t], dst_ref=hagg.at[me],
            send_sem=sa.at[k], recv_sem=ra.at[k], device_id=where(t), device_id_type=MESH)

    @pl.loop(1, n)
    def _(k):
        data_copy(k, tab1, s1, r1).start()

    @pl.loop(1, n)
    def _(k):
        agg_copy(k).start()

    hagg[me] = aggpack[me]
    for j in range(mb):
        tab1[nb + me * mb + j] = pack[me * mb + j]

    @pl.loop(0, nb)
    def _(b):
        tab1[b] = guess[b].astype(bf16)
        dcol[b] = column_of(deg, b)

    weights_copy.wait()

    @pl.loop(1, n)
    def _(k):
        data_copy(k, tab1, s1, r1).wait_recv()

    half = slots // 2

    def off(tab, b):
        low = half_product(w, tab, cols, b, 0, half)
        high = half_product(w, tab, cols, b, half, slots - half)
        return low + jnp.where(counts[b] > half, high, 0.0)

    @pl.loop(0, nb)
    def _(b):
        d, g = dcol[b], guess[b]
        first = g + damping * (rhs[b] - (d * g - off(tab1, b))) / d
        x1[b] = first
        tab2[b] = first.astype(bf16)

    @pl.loop(1, n)
    def _(k):
        data_copy(k, tab1, s1, r1).wait_send()
        agg_copy(k).wait()

    @pl.loop(0, n * mb)
    def _(i):
        pack[i] = x1[sends[i]].astype(bf16)

    @pl.loop(1, n)
    def _(k):
        data_copy(k, tab2, s2, r2).start()

    for j in range(mb):
        tab2[nb + me * mb + j] = pack[me * mb + j]
    hagg_out[...] = hagg[...]

    @pl.loop(1, n)
    def _(k):
        data_copy(k, tab2, s2, r2).wait_recv()

    out_copy = pltpu.make_async_copy(tab2, tab_out, osem)
    out_copy.start()

    @pl.loop(0, nb)
    def _(b):
        res[b] = rhs[b] - (dcol[b] * x1[b] - off(tab2, b))

    @pl.loop(1, n)
    def _(k):
        data_copy(k, tab2, s2, r2).wait_send()

    out_copy.wait()


def restrict_kernel(ways, agg, inv, res, out, *accs):
    for acc in accs:
        acc[...] = jnp.zeros_like(acc)
    span = res.shape[0] // ways
    step = 4

    @pl.loop(0, span // step)
    def _(i):
        for u in range(step):
            for q in range(ways):
                v = q * span + i * step + u
                a = agg[v]
                accs[q][pl.ds(a, 1), :] += res[pl.ds(v, 1), :] * inv[a]

    tile = 64

    @pl.loop(0, out.shape[0] // tile)
    def _(i):
        rows = pl.ds(i * tile, tile)
        total = accs[0][rows, :]
        for acc in accs[1:]:
            total = total + acc[rows, :]
        out[rows, :] = total


def coarse_kernel(nr, nz, parts, orders, coarse, out, acc, sbuf, rbuf, corr, ss, rs, sg, rg):
    nc = coarse.shape[0]
    top = nc // 2
    r, z = lax.axis_index("rows"), lax.axis_index("cores")
    barrier = pltpu.get_barrier_semaphore()

    def partner(bit):
        axis, m = bit
        other = 1 - 2 * lax.rem((r if axis == 0 else z) // m, 2)
        return (r + other * m, z) if axis == 0 else (r, z + other * m)

    def mine(bit):
        axis, m = bit
        return lax.rem((r if axis == 0 else z) // m, 2)

    every = orders[0]
    for bit in every:
        pl.semaphore_signal(barrier, 1, device_id=partner(bit), device_id_type=MESH)
    pl.semaphore_wait(barrier, len(every))

    levels, count = len(every), len(parts)
    base = [sum(parts[:p]) for p in range(count)]
    room, at = [], 0
    for s in range(levels):
        row = []
        for p in range(count):
            size = parts[p] >> s
            row.append((at, size))
            at += size
        room.append(row)

    def sized(size):
        tile = 64
        while size % tile:
            tile //= 2
        return tile

    def rows_of(start, tile, i):
        return pl.ds(pl.multiple_of(start + i * tile, 16), tile)

    def hop(s, p):
        at, size = room[s][p]
        return pltpu.make_async_remote_copy(
            src_ref=sbuf.at[pl.ds(at, size)], dst_ref=rbuf.at[pl.ds(at, size)],
            send_sem=ss.at[s * count + p], recv_sem=rs.at[s * count + p],
            device_id=partner(orders[p][s]), device_id_type=MESH)

    place = list(base)
    for s in range(levels):
        for p in range(count):
            bit = mine(orders[p][s])
            at, size = room[s][p]
            tile = sized(size)
            if s == 0:
                keep, give, source = bit * top + base[p], (1 - bit) * top + base[p], coarse
            else:
                old_at, old_size = room[s - 1][p]
                hop(s - 1, p).wait_recv()
                was = place[p]
                keep, give, source = was + bit * size, was + (1 - bit) * size, acc
                held = coarse if s == 1 else acc
                shift = mine(orders[p][0]) * top if s == 1 else 0
                old_tile = sized(old_size)

                @pl.loop(0, old_size // old_tile)
                def _(i):
                    rows = rows_of(was, old_tile, i)
                    acc[rows, :] = held[rows_of(was + shift, old_tile, i), :] + rbuf[
                        rows_of(old_at, old_tile, i), :].astype(f32)

                place[p] = keep

            @pl.loop(0, size // tile)
            def _(i):
                sbuf[rows_of(at, tile, i), :] = source[rows_of(give, tile, i), :].astype(bf16)

            hop(s, p).start()

    def spread(s, p, start):
        size = parts[p] >> s
        rows = pl.ds(pl.multiple_of(start, 16), size)
        return pltpu.make_async_remote_copy(
            src_ref=corr.at[rows], dst_ref=corr.at[rows],
            send_sem=sg.at[s * count + p], recv_sem=rg.at[s * count + p],
            device_id=partner(orders[p][s]), device_id_type=MESH)

    shift = mine(every[0]) * top
    sent = []
    for s in reversed(range(levels)):
        for p in range(count):
            if s == levels - 1:
                hop(s, p).wait_recv()
                at, size = room[s][p]
                tile = sized(size)
                was = place[p]

                @pl.loop(0, size // tile)
                def _(i):
                    corr[rows_of(was + shift, tile, i), :] = (
                        acc[rows_of(was, tile, i), :] + rbuf[rows_of(at, tile, i), :].astype(f32)
                    ).astype(bf16)
            else:
                sent[-count].wait_recv()
                place[p] = place[p] - mine(orders[p][s + 1]) * (parts[p] >> (s + 1))
            copy = spread(s, p, place[p] + shift)
            copy.start()
            sent.append(copy)

    for copy in sent[-count:]:
        copy.wait_recv()
    for copy in sent:
        copy.wait_send()
    for s in range(levels):
        for p in range(count):
            hop(s, p).wait_send()

    @pl.loop(0, nc // 128)
    def _(i):
        rows = pl.ds(i * 128, 128)
        out[rows, :] = corr[rows, :]


def smooth_kernel(corr, agg, hagg, x1tab, x1, rhs, deg, cols, counts, w_hbm, out,
                  w, fine, tab, x2, tmp, wsem):
    nb, slots, size = w.shape[0], w.shape[1], w.shape[2]
    weights_copy = pltpu.make_async_copy(w_hbm, w, wsem)
    weights_copy.start()

    @pl.loop(0, corr.shape[0] // 128)
    def _(i):
        rows = pl.ds(i * 128, 128)
        fine[rows, :] = corr[rows, :].astype(f32)

    step = 32

    def gather(ids, block):
        @pl.loop(0, size // step)
        def _(i):
            for u in range(step):
                v = i * step + u
                tmp[pl.ds(v, 1), :] = fine[pl.ds(ids[block * size + v], 1), :]

    @pl.loop(0, nb)
    def _(b):
        gather(agg, b)
        second = x1[b] + tmp[...]
        x2[b] = second
        tab[b] = second.astype(bf16)

    @pl.loop(0, tab.shape[0] - nb)
    def _(i):
        gather(hagg, i)
        tab[nb + i] = (x1tab[nb + i].astype(f32) + tmp[...]).astype(bf16)

    weights_copy.wait()
    half = slots // 2

    @pl.loop(0, nb)
    def _(b):
        tmp[...] = half_product(w, tab, cols, b, 0, half)

        @pl.when(counts[b] > half)
        def _():
            tmp[...] += half_product(w, tab, cols, b, half, slots - half)

        d, second = column_of(deg, b), x2[b]
        out[b] = second + damping * (rhs[b] - (d * second - tmp[...])) / d


def halve_orders(nr, nz):
    row_bits = [(0, 1 << k) for k in range(1, nr.bit_length() - 1)]
    z_bits = [(1, 1 << k) for k in range(nz.bit_length() - 1)]
    core = [(0, 1)]
    return [core + row_bits + z_bits, core + row_bits[::-1] + z_bits, core + z_bits + row_bits]


def body(nr, nz, rhs, guess, degree, weights, columns, block_counts, send_lists, aggregates, coarse_diag):
    n = nr * nz
    nb, slots, bs = weights.shape[0], weights.shape[1], weights.shape[2]
    width = rhs.shape[1]
    nc = coarse_diag.shape[0]
    mb = send_lists.shape[2]
    nt = nb + n * mb
    dma = pltpu.SemaphoreType.DMA
    rhs3, guess3 = rhs.reshape(nb, bs, width), guess.reshape(nb, bs, width)
    deg2, agg2 = degree.reshape(nb, bs), aggregates.reshape(nb, bs)
    field = jax.ShapeDtypeStruct((nb, bs, width), f32)

    x1, res, x1tab, hagg = pl.pallas_call(
        functools.partial(relax_kernel, nr, nz),
        out_shape=(field, field, jax.ShapeDtypeStruct((nt, bs, width), bf16),
                   jax.ShapeDtypeStruct((n, mb, bs), i32)),
        in_specs=[VM, VM, VM, VM, SM, SM, SM, ANY],
        out_specs=(VM, VM, ANY, VM),
        scratch_shapes=[
            pltpu.VMEM((nb, slots, bs, bs), bf16),
            pltpu.VMEM((nt, bs, width), bf16),
            pltpu.VMEM((nt, bs, width), bf16),
            pltpu.VMEM((n * mb, bs, width), bf16),
            pltpu.VMEM((n, mb, bs), i32),
            pltpu.VMEM((n, mb, bs), i32),
            pltpu.VMEM((nb, bs, width), f32),
            dma, dma, dma((n,)), dma((n,)), dma((n,)), dma((n,)), dma((n,)), dma((n,)),
        ],
        compiler_params=pltpu.CompilerParams(
            collective_id=1, has_side_effects=True, vmem_limit_bytes=LIMIT),
        name="relax",
    )(guess3, rhs3, deg2, agg2, columns, block_counts, send_lists.reshape(-1), weights)

    ways = 4
    local_coarse = pl.pallas_call(
        functools.partial(restrict_kernel, ways),
        out_shape=jax.ShapeDtypeStruct((nc, width), f32),
        in_specs=[SM, SM, VM],
        out_specs=VM,
        scratch_shapes=[pltpu.VMEM((nc, width), f32)] * ways,
        compiler_params=pltpu.CompilerParams(vmem_limit_bytes=LIMIT),
        name="restrict",
    )(aggregates, 1.0 / coarse_diag, res.reshape(nb * bs, width))

    orders = halve_orders(nr, nz)
    top = nc // 2
    unit = 16 * (n // 2)
    units = top // unit
    parts = [(units + 2) // 3 * unit, (units + 1) // 3 * unit, units // 3 * unit]
    levels = len(orders[0])
    moved = sum(size >> s for s in range(levels) for size in parts)
    sems = dma((levels * 3,))
    correction = pl.pallas_call(
        functools.partial(coarse_kernel, nr, nz, parts, orders),
        out_shape=jax.ShapeDtypeStruct((nc, width), bf16),
        in_specs=[VM],
        out_specs=VM,
        scratch_shapes=[
            pltpu.VMEM((top, width), f32),
            pltpu.VMEM((moved, width), bf16),
            pltpu.VMEM((moved, width), bf16),
            pltpu.VMEM((nc, width), bf16),
            sems, sems, sems, sems,
        ],
        compiler_params=pltpu.CompilerParams(
            collective_id=2, has_side_effects=True, vmem_limit_bytes=LIMIT),
        name="coarse",
    )(local_coarse)

    out = pl.pallas_call(
        smooth_kernel,
        out_shape=field,
        in_specs=[VM, SM, SM, VM, VM, VM, VM, SM, SM, ANY],
        out_specs=VM,
        scratch_shapes=[
            pltpu.VMEM((nb, slots, bs, bs), bf16),
            pltpu.VMEM((nc, width), f32),
            pltpu.VMEM((nt, bs, width), bf16),
            pltpu.VMEM((nb, bs, width), f32),
            pltpu.VMEM((bs, width), f32),
            dma,
        ],
        compiler_params=pltpu.CompilerParams(vmem_limit_bytes=LIMIT),
        name="smooth",
    )(correction, aggregates, hagg.reshape(-1), x1tab, x1, rhs3, deg2, columns, block_counts, weights)
    return out.reshape(nb * bs, width)


def solution(mesh):
    both = ("rows", "cores")
    return jax.shard_map(
        functools.partial(body, mesh.shape["rows"], mesh.shape["cores"]),
        mesh=mesh,
        in_specs=(
            P(both, None), P(both, None), P(both), P(both, None, None, None), P(both, None),
            P(both), P(both, None, None), P(both), P(),
        ),
        out_specs=P(both, None),
        check_vma=False,
    )
```

time: 502 us -> 248 us (0.49)
  Pallas kernels: 0 us -> 242 us
  waiting for transfers between devices: 226 us -> 0 us
  blocking collectives: 104 us -> 0 us
  local copies, waits for them, and re-layouts: 64.6 us -> 2.72 us
  other arithmetic: 45.8 us -> 1.48 us
  matrix products: 39.3 us -> 0 us
  between operations: 13.6 us -> 0.02 us
  starting transfers between devices: 7.37 us -> 0 us
    pallas_call x0 -> x4, Pallas kernels: none -> 242 us  [the longest x1 124 us: body(): pl.pallas_call(functools.partial(relax_kernel, nr, nz), out_shape=(field,...]
    psum x1 -> x0, waiting for transfers between devices: 179 us -> none  [body(): total = lax.psum(local_coarse, ('rows', 'cores'))]
    all_to_all x2 -> x0, blocking collectives: 104 us -> none  [apply(): lax.all_to_all(outgoing, ('rows', 'cores'), split_axis=0, concat_axis=0,...]
    gather x7 -> x0, local copies, waits for them, and re-layouts: 62.9 us -> none  [the longest x3 41.8 us: apply(): table[columns]]
    all_to_all x1 -> x0, waiting for transfers between devices: 46.6 us -> none  [apply(): lax.all_to_all(outgoing, ('rows', 'cores'), split_axis=0, concat_axis=0,...]
    dot_general x3 -> x0, matrix products: 39.3 us -> none  [apply(): jnp.einsum('bsij,bsjr->bir', live_weights, table[columns], preferred_elem...]
    scatter-add x1 -> x0, other arithmetic: 26.4 us -> none  [body(): local_coarse = jax.ops.segment_sum(residue, aggregates, num_segments=NC)]
    convert_element_type x5 -> x0, other arithmetic: 12 us -> none  [the longest x1 6.87 us: body(): correction = (total / coarse_diag[:, None]).astype(jnp.bfloat16)]
  transfers between devices with their start and end apart: 2 -> 0, of which waited for: 2 -> 0; matrix products, arithmetic and copies ran while one was open for 0% -> 0% of each run, Pallas kernels for 0% -> 0%
where the time goes in v1:
time: 248 us; the launch traced here: 247 us
  Pallas kernels  242 us (98%)
  local copies, waits for them, and re-layouts  2.72 us (1%)
    pallas_call x1, Pallas kernels, body(): pl.pallas_call(functools.partial(relax_kernel, nr, nz), out_shape=(field,...  124 us
    pallas_call x1, Pallas kernels, body(): pl.pallas_call(functools.partial(coarse_kernel, nr, nz, parts, orders), o...  66.5 us
    pallas_call x1, Pallas kernels, body(): pl.pallas_call(smooth_kernel, out_shape=field, in_specs=[VM, SM, SM, VM,...  34.8 us
    pallas_call x1, Pallas kernels, body(): pl.pallas_call(functools.partial(restrict_kernel, ways), out_shape=jax.Sh...  17.1 us

profile of v1, /device:TPU:0, one launch (start us, length us, event | category | flops | bytes accessed | tf_op | source)
XLA Modules:
  0.0 246.5 jit_solution(8183210633162549080)
XLA Ops:
  0.0 1.4 copy.14.cols
  1.4 0.8 copy.13
  2.1 0.6 reshape.28.sends
  2.7 1.5 broadcast_divide_fusion.inv
  4.2 124.0 %relax.1 = (f32[32,128,128]{2,1,0:T(8,128)}, f32[32,128,128]{2,1,0:T(8,128)}, bf16[96,128,128]{2,1,0:T(8,128)(2,1)}, s32[32,2,128]{2,1,0:T(2,128)}) custom-call(f32[32,128,128]{2,1,0:T(8,128)} %bitcast.9, f32[32,128,128]{2,1,0:T(8,128)} %bitcast.7, f32[32,128]{1,0:T(8,128)} %bitcast.12, s32[32,128]{1,0:T(8,128)} %bitcast.11, s32[32,16]{1,0:T(8,128)} %copy.14.cols, ...), custom_call_target="tpu_custom_call" | custom-call | tf_op jit(solution)/shard_map/relax/pallas_call | solution.py:355
  128.2 17.1 %restrict.1.coarse = f32[16384,128]{1,0:T(8,128)} custom-call(s32[4096]{0:T(1024)} %agg.3, f32[16384]{0:T(1024)} %broadcast_divide_fusion.inv, f32[4096,128]{1,0:T(8,128)} %bitcast.10), custom_call_target="tpu_custom_call" | custom-call | tf_op jit(solution)/shard_map/restrict/pallas_call | solution.py:377
  145.3 66.5 %coarse.1.corr = bf16[16384,128]{1,0:T(8,128)(2,1)} custom-call(f32[16384,128]{1,0:T(8,128)} %restrict.1.coarse), custom_call_target="tpu_custom_call" | custom-call | tf_op jit(solution)/shard_map/coarse/pallas_call | solution.py:395
  211.8 34.8 %smooth.1 = f32[32,128,128]{2,1,0:T(8,128)} custom-call(bf16[16384,128]{1,0:T(8,128)(2,1)} %coarse.1.corr, s32[4096]{0:T(1024)} %agg.3, s32[8192]{0:T(1024)} %bitcast.14, bf16[96,128,128]{2,1,0:T(8,128)(2,1)} %get-tuple-element.11.x1tab, f32[32,128,128]{2,1,0:T(8,128)} %get-tuple-element.12.x1, f32[32,128,128]{2,1,0:T(8,128)} %bitcast.8, ...), custom_call_target="tpu_custom_call" | custom-call | tf_op jit(solution)/shard_map/smooth/pallas_call | solution.py:412

commit v2 on v1

--- a/solution.py
+++ b/solution.py
@@ -20,18 +20,26 @@
     return jnp.transpose(jnp.broadcast_to(row, (row.shape[1], row.shape[1])))
 
 
-def half_product(w, tab, cols, b, first, count):
-    left = jnp.concatenate([w[b, first + s] for s in range(count)], axis=1)
-    right = jnp.concatenate([tab[cols[b, first + s]] for s in range(count)], axis=0)
+def row_product(w, tab, cols, b):
+    slots = w.shape[1]
+    left = jnp.concatenate([w[b, s] for s in range(slots)], axis=1)
+    right = jnp.concatenate([tab[cols[s, b]] for s in range(slots)], axis=0)
     return jnp.dot(left, right, preferred_element_type=f32)
 
 
-def relax_kernel(nr, nz, guess, rhs, deg, agg, cols, counts, sends, w_hbm,
+def each_row(count, step, act):
+    @pl.loop(0, count // step)
+    def _(i):
+        for u in range(step):
+            act(i * step + u)
+
+
+def relax_kernel(nr, nz, guess, rhs_hbm, deg, agg, cols, sends, w_hbm,
                  x1, res, tab_out, hagg_out,
-                 w, tab1, tab2, pack, aggpack, hagg, dcol,
-                 wsem, osem, s1, r1, s2, r2, sa, ra):
+                 w, tab1, tab2, pack, aggpack, hagg, dcol, rhs,
+                 wsem, bsem, osem, s1, r1, s2, r2, sa, ra):
     n = nr * nz
-    nb, slots = w.shape[0], w.shape[1]
+    nb = w.shape[0]
     mb = pack.shape[0] // n
     me = lax.axis_index("rows") * nz + lax.axis_index("cores")
     barrier = pltpu.get_barrier_semaphore()
@@ -44,12 +52,14 @@
         pl.semaphore_signal(barrier, 1, device_id=where(lax.rem(me + k, n)), device_id_type=MESH)
 
     weights_copy = pltpu.make_async_copy(w_hbm, w, wsem)
+    rhs_copy = pltpu.make_async_copy(rhs_hbm, rhs, bsem)
     weights_copy.start()
+    rhs_copy.start()
 
     @pl.loop(0, n)
     def _(t):
         for j in range(mb):
-            b = sends[t * mb + j]
+            b = sends[j, t]
             pack[t * mb + j] = guess[b].astype(bf16)
             aggpack[t, pl.ds(j, 1), :] = agg[pl.ds(b, 1), :]
 
@@ -84,34 +94,32 @@
         tab1[b] = guess[b].astype(bf16)
         dcol[b] = column_of(deg, b)
 
+    for tab in (tab1, tab2):
+        tab[nb + n * mb] = jnp.zeros(tab.shape[1:], bf16)
     weights_copy.wait()
+    rhs_copy.wait()
 
     @pl.loop(1, n)
     def _(k):
         data_copy(k, tab1, s1, r1).wait_recv()
 
-    half = slots // 2
-
-    def off(tab, b):
-        low = half_product(w, tab, cols, b, 0, half)
-        high = half_product(w, tab, cols, b, half, slots - half)
-        return low + jnp.where(counts[b] > half, high, 0.0)
-
-    @pl.loop(0, nb)
-    def _(b):
+    def sweep(b):
         d, g = dcol[b], guess[b]
-        first = g + damping * (rhs[b] - (d * g - off(tab1, b))) / d
+        first = g + damping * (rhs[b] - (d * g - row_product(w, tab1, cols, b))) / d
         x1[b] = first
         tab2[b] = first.astype(bf16)
 
+    each_row(nb, 4, sweep)
+
     @pl.loop(1, n)
     def _(k):
         data_copy(k, tab1, s1, r1).wait_send()
         agg_copy(k).wait()
 
-    @pl.loop(0, n * mb)
-    def _(i):
-        pack[i] = x1[sends[i]].astype(bf16)
+    @pl.loop(0, n)
+    def _(t):
+        for j in range(mb):
+            pack[t * mb + j] = x1[sends[j, t]].astype(bf16)
 
     @pl.loop(1, n)
     def _(k):
@@ -128,9 +136,10 @@
     out_copy = pltpu.make_async_copy(tab2, tab_out, osem)
     out_copy.start()
 
-    @pl.loop(0, nb)
-    def _(b):
-        res[b] = rhs[b] - (dcol[b] * x1[b] - off(tab2, b))
+    def residue(b):
+        res[b] = rhs[b] - (dcol[b] * x1[b] - row_product(w, tab2, cols, b))
+
+    each_row(nb, 4, residue)
 
     @pl.loop(1, n)
     def _(k):
@@ -139,32 +148,46 @@
     out_copy.wait()
 
 
-def restrict_kernel(ways, agg, inv, res, out, *accs):
+def restrict_kernel(ways, agg, inv, res, out, *scratch):
+    accs, sem = scratch[:ways], scratch[ways]
     for acc in accs:
         acc[...] = jnp.zeros_like(acc)
     span = res.shape[0] // ways
-    step = 4
+    step = 8
 
     @pl.loop(0, span // step)
     def _(i):
         for u in range(step):
+            places = [agg[q * span + i * step + u] for q in range(ways)]
+            sums = [
+                accs[q][pl.ds(places[q], 1), :]
+                + res[pl.ds(q * span + i * step + u, 1), :] * inv[places[q]]
+                for q in range(ways)
+            ]
             for q in range(ways):
-                v = q * span + i * step + u
-                a = agg[v]
-                accs[q][pl.ds(a, 1), :] += res[pl.ds(v, 1), :] * inv[a]
-
-    tile = 64
-
-    @pl.loop(0, out.shape[0] // tile)
-    def _(i):
-        rows = pl.ds(i * tile, tile)
-        total = accs[0][rows, :]
-        for acc in accs[1:]:
-            total = total + acc[rows, :]
-        out[rows, :] = total
-
-
-def coarse_kernel(nr, nz, parts, orders, coarse, out, acc, sbuf, rbuf, corr, ss, rs, sg, rg):
+                accs[q][pl.ds(places[q], 1), :] = sums[q]
+
+    tile, pieces = 64, 8
+    piece = out.shape[0] // pieces
+    copies = []
+    for c in range(pieces):
+        @pl.loop(0, piece // tile)
+        def _(i):
+            rows = pl.ds(c * piece + i * tile, tile)
+            total = accs[0][rows, :]
+            for acc in accs[1:]:
+                total = total + acc[rows, :]
+            accs[0][rows, :] = total
+
+        rows = pl.ds(c * piece, piece)
+        copy = pltpu.make_async_copy(accs[0].at[rows], out.at[rows], sem.at[c])
+        copy.start()
+        copies.append(copy)
+    for copy in copies:
+        copy.wait()
+
+
+def coarse_kernel(nr, nz, parts, orders, coarse_hbm, out, coarse, acc, sbuf, rbuf, corr, ss, rs, sg, rg, load, store):
     nc = coarse.shape[0]
     top = nc // 2
     r, z = lax.axis_index("rows"), lax.axis_index("cores")
@@ -180,12 +203,22 @@
         return lax.rem((r if axis == 0 else z) // m, 2)
 
     every = orders[0]
+    count = len(parts)
+    base = [sum(parts[:p]) for p in range(count)]
+    loads = []
+    for side in range(2):
+        for p in range(count):
+            start = lax.rem(1 - mine(every[0]) + side, 2) * top + base[p]
+            rows = pl.ds(pl.multiple_of(start, 16), parts[p])
+            copy = pltpu.make_async_copy(coarse_hbm.at[rows], coarse.at[rows], load.at[side * count + p])
+            copy.start()
+            loads.append(copy)
+
     for bit in every:
         pl.semaphore_signal(barrier, 1, device_id=partner(bit), device_id_type=MESH)
     pl.semaphore_wait(barrier, len(every))
 
-    levels, count = len(every), len(parts)
-    base = [sum(parts[:p]) for p in range(count)]
+    levels = len(every)
     room, at = [], 0
     for s in range(levels):
         row = []
@@ -218,10 +251,13 @@
             at, size = room[s][p]
             tile = sized(size)
             if s == 0:
+                loads[p].wait()
                 keep, give, source = bit * top + base[p], (1 - bit) * top + base[p], coarse
             else:
                 old_at, old_size = room[s - 1][p]
                 hop(s - 1, p).wait_recv()
+                if s == 1:
+                    loads[count + p].wait()
                 was = place[p]
                 keep, give, source = was + bit * size, was + (1 - bit) * size, acc
                 held = coarse if s == 1 else acc
@@ -272,72 +308,80 @@
             copy.start()
             sent.append(copy)
 
-    for copy in sent[-count:]:
-        copy.wait_recv()
+    def flush(start, size, index):
+        rows = pl.ds(pl.multiple_of(start, 16), size)
+        return pltpu.make_async_copy(corr.at[rows], out.at[rows], store.at[index])
+
+    flushes = [flush(shift, top, 0)]
+    flushes[0].start()
+    for p in range(count):
+        sent[p - count].wait_recv()
+        flushes.append(flush(top - shift + base[p], parts[p], 1 + p))
+        flushes[-1].start()
     for copy in sent:
         copy.wait_send()
     for s in range(levels):
         for p in range(count):
             hop(s, p).wait_send()
 
-    @pl.loop(0, nc // 128)
-    def _(i):
-        rows = pl.ds(i * 128, 128)
-        out[rows, :] = corr[rows, :]
-
-
-def smooth_kernel(corr, agg, hagg, x1tab, x1, rhs, deg, cols, counts, w_hbm, out,
-                  w, fine, tab, x2, tmp, wsem):
-    nb, slots, size = w.shape[0], w.shape[1], w.shape[2]
-    weights_copy = pltpu.make_async_copy(w_hbm, w, wsem)
-    weights_copy.start()
+    for copy in flushes:
+        copy.wait()
+
+
+def smooth_kernel(corr, agg, hagg, x1tab, x1_hbm, rhs_hbm, deg, cols, w_hbm, out,
+                  w, fine, tab, x2, rhs, sems):
+    nb, size = w.shape[0], w.shape[2]
+    pairs = ((x1tab, tab), (x1_hbm, x2), (w_hbm, w), (rhs_hbm, rhs))
+    copies = [pltpu.make_async_copy(a, b, sems.at[k]) for k, (a, b) in enumerate(pairs)]
+    for copy in copies:
+        copy.start()
 
     @pl.loop(0, corr.shape[0] // 128)
     def _(i):
         rows = pl.ds(i * 128, 128)
         fine[rows, :] = corr[rows, :].astype(f32)
 
-    step = 32
-
-    def gather(ids, block):
-        @pl.loop(0, size // step)
-        def _(i):
-            for u in range(step):
-                v = i * step + u
-                tmp[pl.ds(v, 1), :] = fine[pl.ds(ids[block * size + v], 1), :]
+    copies[0].wait()
+    copies[1].wait()
+    step = 16
+
+    def gathered(ids, first):
+        return jnp.concatenate([fine[pl.ds(ids[first + u], 1), :] for u in range(step)], axis=0)
 
     @pl.loop(0, nb)
     def _(b):
-        gather(agg, b)
-        second = x1[b] + tmp[...]
-        x2[b] = second
-        tab[b] = second.astype(bf16)
-
-    @pl.loop(0, tab.shape[0] - nb)
-    def _(i):
-        gather(hagg, i)
-        tab[nb + i] = (x1tab[nb + i].astype(f32) + tmp[...]).astype(bf16)
-
-    weights_copy.wait()
-    half = slots // 2
-
-    @pl.loop(0, nb)
+        for i in range(size // step):
+            rows = slice(i * step, (i + 1) * step)
+            second = x2[b, rows, :] + gathered(agg, b * size + i * step)
+            x2[b, rows, :] = second
+            tab[b, rows, :] = second.astype(bf16)
+
+    @pl.loop(nb, tab.shape[0] - 1)
     def _(b):
-        tmp[...] = half_product(w, tab, cols, b, 0, half)
-
-        @pl.when(counts[b] > half)
-        def _():
-            tmp[...] += half_product(w, tab, cols, b, half, slots - half)
-
+        for i in range(size // step):
+            rows = slice(i * step, (i + 1) * step)
+            moved = tab[b, rows, :].astype(f32) + gathered(hagg, (b - nb) * size + i * step)
+            tab[b, rows, :] = moved.astype(bf16)
+
+    copies[2].wait()
+    copies[3].wait()
+
+    def finish(b):
         d, second = column_of(deg, b), x2[b]
-        out[b] = second + damping * (rhs[b] - (d * second - tmp[...])) / d
+        out[b] = second + damping * (rhs[b] - (d * second - row_product(w, tab, cols, b))) / d
+
+    each_row(nb, 4, finish)
 
 
 def halve_orders(nr, nz):
     row_bits = [(0, 1 << k) for k in range(1, nr.bit_length() - 1)]
     z_bits = [(1, 1 << k) for k in range(nz.bit_length() - 1)]
     core = [(0, 1)]
-    return [core + row_bits + z_bits, core + row_bits[::-1] + z_bits, core + z_bits + row_bits]
+    return 2 * [
+        core + row_bits[:1] + z_bits[:1] + row_bits[1:] + z_bits[1:],
+        core + row_bits[::-1] + z_bits,
+        core + z_bits + row_bits,
+    ]
 
 
 def body(nr, nz, rhs, guess, degree, weights, columns, block_counts, send_lists, aggregates, coarse_diag):
@@ -346,17 +390,19 @@
     width = rhs.shape[1]
     nc = coarse_diag.shape[0]
     mb = send_lists.shape[2]
-    nt = nb + n * mb
+    nt = nb + n * mb + 1
     dma = pltpu.SemaphoreType.DMA
     rhs3, guess3 = rhs.reshape(nb, bs, width), guess.reshape(nb, bs, width)
     deg2, agg2 = degree.reshape(nb, bs), aggregates.reshape(nb, bs)
+    live = jnp.arange(slots, dtype=i32)[:, None] < block_counts[None, :]
+    cols = jnp.where(live, columns.T, nt - 1)
     field = jax.ShapeDtypeStruct((nb, bs, width), f32)
 
     x1, res, x1tab, hagg = pl.pallas_call(
         functools.partial(relax_kernel, nr, nz),
         out_shape=(field, field, jax.ShapeDtypeStruct((nt, bs, width), bf16),
                    jax.ShapeDtypeStruct((n, mb, bs), i32)),
-        in_specs=[VM, VM, VM, VM, SM, SM, SM, ANY],
+        in_specs=[VM, ANY, VM, VM, SM, SM, ANY],
         out_specs=(VM, VM, ANY, VM),
         scratch_shapes=[
             pltpu.VMEM((nb, slots, bs, bs), bf16),
@@ -366,20 +412,21 @@
             pltpu.VMEM((n, mb, bs), i32),
             pltpu.VMEM((n, mb, bs), i32),
             pltpu.VMEM((nb, bs, width), f32),
-            dma, dma, dma((n,)), dma((n,)), dma((n,)), dma((n,)), dma((n,)), dma((n,)),
+            pltpu.VMEM((nb, bs, width), f32),
+            dma, dma, dma, dma((n,)), dma((n,)), dma((n,)), dma((n,)), dma((n,)), dma((n,)),
         ],
         compiler_params=pltpu.CompilerParams(
             collective_id=1, has_side_effects=True, vmem_limit_bytes=LIMIT),
         name="relax",
-    )(guess3, rhs3, deg2, agg2, columns, block_counts, send_lists.reshape(-1), weights)
+    )(guess3, rhs3, deg2, agg2, cols, send_lists[0].T, weights)
 
     ways = 4
     local_coarse = pl.pallas_call(
         functools.partial(restrict_kernel, ways),
         out_shape=jax.ShapeDtypeStruct((nc, width), f32),
         in_specs=[SM, SM, VM],
-        out_specs=VM,
-        scratch_shapes=[pltpu.VMEM((nc, width), f32)] * ways,
+        out_specs=ANY,
+        scratch_shapes=[pltpu.VMEM((nc, width), f32)] * ways + [dma((8,))],
         compiler_params=pltpu.CompilerParams(vmem_limit_bytes=LIMIT),
         name="restrict",
     )(aggregates, 1.0 / coarse_diag, res.reshape(nb * bs, width))
@@ -388,21 +435,23 @@
     top = nc // 2
     unit = 16 * (n // 2)
     units = top // unit
-    parts = [(units + 2) // 3 * unit, (units + 1) // 3 * unit, units // 3 * unit]
+    count = len(orders)
+    parts = [(units + count - 1 - p) // count * unit for p in range(count)]
     levels = len(orders[0])
     moved = sum(size >> s for s in range(levels) for size in parts)
-    sems = dma((levels * 3,))
+    sems = dma((levels * count,))
     correction = pl.pallas_call(
         functools.partial(coarse_kernel, nr, nz, parts, orders),
         out_shape=jax.ShapeDtypeStruct((nc, width), bf16),
-        in_specs=[VM],
-        out_specs=VM,
+        in_specs=[ANY],
+        out_specs=ANY,
         scratch_shapes=[
+            pltpu.VMEM((nc, width), f32),
             pltpu.VMEM((top, width), f32),
             pltpu.VMEM((moved, width), bf16),
             pltpu.VMEM((moved, width), bf16),
             pltpu.VMEM((nc, width), bf16),
-            sems, sems, sems, sems,
+            sems, sems, sems, sems, dma((2 * count,)), dma((count + 1,)),
         ],
         compiler_params=pltpu.CompilerParams(
             collective_id=2, has_side_effects=True, vmem_limit_bytes=LIMIT),
@@ -412,19 +461,19 @@
     out = pl.pallas_call(
         smooth_kernel,
         out_shape=field,
-        in_specs=[VM, SM, SM, VM, VM, VM, VM, SM, SM, ANY],
+        in_specs=[VM, SM, SM, ANY, ANY, ANY, VM, SM, ANY],
         out_specs=VM,
         scratch_shapes=[
             pltpu.VMEM((nb, slots, bs, bs), bf16),
             pltpu.VMEM((nc, width), f32),
             pltpu.VMEM((nt, bs, width), bf16),
             pltpu.VMEM((nb, bs, width), f32),
-            pltpu.VMEM((bs, width), f32),
-            dma,
+            pltpu.VMEM((nb, bs, width), f32),
+            dma((4,)),
         ],
         compiler_params=pltpu.CompilerParams(vmem_limit_bytes=LIMIT),
         name="smooth",
-    )(correction, aggregates, hagg.reshape(-1), x1tab, x1, rhs3, deg2, columns, block_counts, weights)
+    )(correction, aggregates, hagg.reshape(-1), x1tab, x1, rhs3, deg2, cols, weights)
     return out.reshape(nb * bs, width)
 
 

time: 248 us -> 209 us (0.84)
  Pallas kernels: 242 us -> 206 us
  local copies, waits for them, and re-layouts: 2.72 us -> 0 us
    pallas_call x1, Pallas kernels: 34.8 us -> 22.3 us  [body(): pl.pallas_call(smooth_kernel, out_shape=field, in_specs=[VM, SM, SM, ANY,...]
    pallas_call x1, Pallas kernels: 66.5 us -> 54.2 us  [body(): pl.pallas_call(functools.partial(coarse_kernel, nr, nz, parts, orders), o...]
    pallas_call x1, Pallas kernels: 124 us -> 116 us  [body(): pl.pallas_call(functools.partial(relax_kernel, nr, nz), out_shape=(field,...]
    pallas_call x1, Pallas kernels: 17.1 us -> 13.9 us  [body(): pl.pallas_call(functools.partial(restrict_kernel, ways), out_shape=jax.Sh...]
where the time goes in v2:
time: 209 us
  Pallas kernels  206 us (99%)
  other arithmetic  2.77 us (1%)
    pallas_call x1, Pallas kernels, body(): pl.pallas_call(functools.partial(relax_kernel, nr, nz), out_shape=(field,...  116 us
    pallas_call x1, Pallas kernels, body(): pl.pallas_call(functools.partial(coarse_kernel, nr, nz, parts, orders), o...  54.2 us
    pallas_call x1, Pallas kernels, body(): pl.pallas_call(smooth_kernel, out_shape=field, in_specs=[VM, SM, SM, ANY,...  22.3 us
    pallas_call x1, Pallas kernels, body(): pl.pallas_call(functools.partial(restrict_kernel, ways), out_shape=jax.Sh...  13.9 us

profile of v2, /device:TPU:0, one launch (start us, length us, event | category | flops | bytes accessed | tf_op | source)
XLA Modules:
  0.0 209.0 jit_solution(2151336710625277470)
XLA Ops:
  0.0 1.3 bitcast_select_fusion.cols
  1.3 1.5 broadcast_divide_fusion.inv
  2.8 115.7 %relax.1 = (f32[32,128,128]{2,1,0:T(8,128)}, f32[32,128,128]{2,1,0:T(8,128)}, bf16[97,128,128]{2,1,0:T(8,128)(2,1)}, s32[32,2,128]{2,1,0:T(2,128)}) custom-call(f32[32,128,128]{2,1,0:T(8,128)} %bitcast.14, f32[32,128,128]{2,1,0:T(8,128)} %bitcast.12, f32[32,128]{1,0:T(8,128)} %bitcast.17, s32[32,128]{1,0:T(8,128)} %bitcast.16, ...), custom_call_target="tpu_custom_call" | custom-call | tf_op jit(solution)/shard_map/relax/pallas_call | solution.py:401
  118.5 13.9 %restrict.1.coarse_hbm = f32[16384,128]{1,0:T(8,128)} custom-call(s32[4096]{0:T(1024)} %agg.3, f32[16384]{0:T(1024)} %broadcast_divide_fusion.inv, f32[4096,128]{1,0:T(8,128)} %bitcast.15), custom_call_target="tpu_custom_call" | custom-call | tf_op jit(solution)/shard_map/restrict/pallas_call | solution.py:424
  132.4 54.2 %coarse.1.corr = bf16[16384,128]{1,0:T(8,128)(2,1)} custom-call(f32[16384,128]{1,0:T(8,128)} %restrict.1.coarse_hbm), custom_call_target="tpu_custom_call" | custom-call | tf_op jit(solution)/shard_map/coarse/pallas_call | solution.py:443
  186.7 22.3 %smooth.1 = f32[32,128,128]{2,1,0:T(8,128)} custom-call(bf16[16384,128]{1,0:T(8,128)(2,1)} %coarse.1.corr, s32[4096]{0:T(1024)} %agg.3, s32[8192]{0:T(1024)} %bitcast.19, bf16[97,128,128]{2,1,0:T(8,128)(2,1)} %get-tuple-element.11.x1tab, f32[32,128,128]{2,1,0:T(8,128)} %get-tuple-element.12.x1_hbm, f32[32,128,128]{2,1,0:T(8,128)} %bitcast.13, ...), custom_call_target="tpu_custom_call" | custom-call | tf_op jit(solution)/shard_map/smooth/pallas_call | solution.py:461

commit v3 on v2

--- a/solution.py
+++ b/solution.py
@@ -35,9 +35,9 @@
 
 
 def relax_kernel(nr, nz, guess, rhs_hbm, deg, agg, cols, sends, w_hbm,
-                 x1, res, tab_out, hagg_out,
-                 w, tab1, tab2, pack, aggpack, hagg, dcol, rhs,
-                 wsem, bsem, osem, s1, r1, s2, r2, sa, ra):
+                 x1_out, res, tab_out, hagg_out,
+                 w, tab1, tab2, pack, aggpack, hagg, dcol, rhs, x1,
+                 wsem, bsem, osem, xsem, s1, r1, s2, r2, sa, ra):
     n = nr * nz
     nb = w.shape[0]
     mb = pack.shape[0] // n
@@ -109,7 +109,9 @@
         x1[b] = first
         tab2[b] = first.astype(bf16)
 
-    each_row(nb, 4, sweep)
+    each_row(nb, 8, sweep)
+    x1_copy = pltpu.make_async_copy(x1, x1_out, xsem)
+    x1_copy.start()
 
     @pl.loop(1, n)
     def _(k):
@@ -139,13 +141,14 @@
     def residue(b):
         res[b] = rhs[b] - (dcol[b] * x1[b] - row_product(w, tab2, cols, b))
 
-    each_row(nb, 4, residue)
+    each_row(nb, 8, residue)
 
     @pl.loop(1, n)
     def _(k):
         data_copy(k, tab2, s2, r2).wait_send()
 
     out_copy.wait()
+    x1_copy.wait()
 
 
 def restrict_kernel(ways, agg, inv, res, out, *scratch):
@@ -370,7 +373,7 @@
         d, second = column_of(deg, b), x2[b]
         out[b] = second + damping * (rhs[b] - (d * second - row_product(w, tab, cols, b))) / d
 
-    each_row(nb, 4, finish)
+    each_row(nb, 8, finish)
 
 
 def halve_orders(nr, nz):
@@ -403,7 +406,7 @@
         out_shape=(field, field, jax.ShapeDtypeStruct((nt, bs, width), bf16),
                    jax.ShapeDtypeStruct((n, mb, bs), i32)),
         in_specs=[VM, ANY, VM, VM, SM, SM, ANY],
-        out_specs=(VM, VM, ANY, VM),
+        out_specs=(ANY, VM, ANY, VM),
         scratch_shapes=[
             pltpu.VMEM((nb, slots, bs, bs), bf16),
             pltpu.VMEM((nt, bs, width), bf16),
@@ -413,7 +416,8 @@
             pltpu.VMEM((n, mb, bs), i32),
             pltpu.VMEM((nb, bs, width), f32),
             pltpu.VMEM((nb, bs, width), f32),
-            dma, dma, dma, dma((n,)), dma((n,)), dma((n,)), dma((n,)), dma((n,)), dma((n,)),
+            pltpu.VMEM((nb, bs, width), f32),
+            dma, dma, dma, dma, dma((n,)), dma((n,)), dma((n,)), dma((n,)), dma((n,)), dma((n,)),
         ],
         compiler_params=pltpu.CompilerParams(
             collective_id=1, has_side_effects=True, vmem_limit_bytes=LIMIT),

time: 209 us -> 207 us (level)
  no operation moved by 1% of the time
where the time goes in v3:
time: 207 us
  Pallas kernels  204 us (99%)
  other arithmetic  2.77 us (1%)
    pallas_call x1, Pallas kernels, body(): pl.pallas_call(functools.partial(relax_kernel, nr, nz), out_shape=(field,...  114 us
    pallas_call x1, Pallas kernels, body(): pl.pallas_call(functools.partial(coarse_kernel, nr, nz, parts, orders), o...  54.2 us
    pallas_call x1, Pallas kernels, body(): pl.pallas_call(smooth_kernel, out_shape=field, in_specs=[VM, SM, SM, ANY,...  21.7 us
    pallas_call x1, Pallas kernels, body(): pl.pallas_call(functools.partial(restrict_kernel, ways), out_shape=jax.Sh...  13.9 us

profile of v3, /device:TPU:0, one launch (start us, length us, event | category | flops | bytes accessed | tf_op | source)
XLA Modules:
  0.0 206.6 jit_solution(17690944471742402466)
XLA Ops:
  0.0 1.3 bitcast_select_fusion.cols
  1.3 1.5 broadcast_divide_fusion.inv
  2.8 114.0 %relax.1 = (f32[32,128,128]{2,1,0:T(8,128)}, f32[32,128,128]{2,1,0:T(8,128)}, bf16[97,128,128]{2,1,0:T(8,128)(2,1)}, s32[32,2,128]{2,1,0:T(2,128)}) custom-call(f32[32,128,128]{2,1,0:T(8,128)} %bitcast.14, f32[32,128,128]{2,1,0:T(8,128)} %bitcast.12, f32[32,128]{1,0:T(8,128)} %bitcast.17, s32[32,128]{1,0:T(8,128)} %bitcast.16, ...), custom_call_target="tpu_custom_call" | custom-call | tf_op jit(solution)/shard_map/relax/pallas_call | solution.py:404
  116.8 13.9 %restrict.1.coarse_hbm = f32[16384,128]{1,0:T(8,128)} custom-call(s32[4096]{0:T(1024)} %agg.3, f32[16384]{0:T(1024)} %broadcast_divide_fusion.inv, f32[4096,128]{1,0:T(8,128)} %bitcast.15), custom_call_target="tpu_custom_call" | custom-call | tf_op jit(solution)/shard_map/restrict/pallas_call | solution.py:428
  130.7 54.2 %coarse.1.corr = bf16[16384,128]{1,0:T(8,128)(2,1)} custom-call(f32[16384,128]{1,0:T(8,128)} %restrict.1.coarse_hbm), custom_call_target="tpu_custom_call" | custom-call | tf_op jit(solution)/shard_map/coarse/pallas_call | solution.py:447
  184.9 21.7 %smooth.1 = f32[32,128,128]{2,1,0:T(8,128)} custom-call(bf16[16384,128]{1,0:T(8,128)(2,1)} %coarse.1.corr, s32[4096]{0:T(1024)} %agg.3, s32[8192]{0:T(1024)} %bitcast.19, bf16[97,128,128]{2,1,0:T(8,128)(2,1)} %get-tuple-element.11.x1tab, f32[32,128,128]{2,1,0:T(8,128)} %get-tuple-element.12.x1_hbm, f32[32,128,128]{2,1,0:T(8,128)} %bitcast.13, ...), custom_call_target="tpu_custom_call" | custom-call | tf_op jit(solution)/shard_map/smooth/pallas_call | solution.py:465
